TPU v7x, 32 devices: a whole 2x2x4 slice. The times are simulated.
32 devices in a mesh: group: 2 (over x), seq: 8 (over z, y), tensor: 2 (over core).
Axes of the slice: x: 2, y: 2, z: 4, core: 2. Of those that a mesh axis runs over, the one named last changes fastest.
Arguments:
- hidden: bfloat16 [6, 1024, 8192], P('group', 'seq', 'tensor'), parts along dimension 0, may hold values from -64 to 64
- norm_gain: bfloat16 [8192], replicated, may hold values from 0.099609375 to 1.8984375
- w_kv: bfloat16 [8192, 1024], P(None, 'tensor'), may hold values from -0.0625 to 0.0625
- lengths: int32 [6], P('group'), parts along dimension 0, may hold values from 512 to 1024
- page_table: int32 [6, 8], P('group', 'seq'), parts along dimension 0, may hold values from 0 to 63, as said below
Outputs:
- kv_cache: bfloat16 [128, 128, 1024], P(('group', 'seq'), None, 'tensor'), parts along dimension 0
There are 2 independent parts, one for each index of `group`. A program takes and returns all parts, laid end to end along the dimension named above; an argument that names none is the same for every part. Nothing has to cross between parts.
Inputs may be any that keep to these rules, and one draw needn't show every extreme that they name: `page_table`: entries are distinct; page p is held by index p // 8 of seq in its slot p % 8. In every draw some index of seq holds 8 pages whose blocks all start below the window's length, and some index of seq sends all its 3 blocks to that one holder.
All inputs are finite; a program needn't handle non-finite values.
Results may differ from a plain program's by a relative error of at most 0.0049.
Values may be sent and summed in bfloat16 or wider, within the bound.
A program may use at most 128 MiB of HBM per device.

v0:
```python
import functools

import jax
import jax.numpy as jnp
import numpy as np
from jax import lax
from jax.experimental import pallas as pl
from jax.experimental.pallas import tpu as pltpu
from jax.sharding import PartitionSpec as P

HD = 128
BLOCK = 128
SLOTS = 8
PIECES = 8
PLANE = 4

epsilon = 1e-05
rope_base = 500000.0
MESH = pl.DeviceIdType.MESH


def kernel(
    depth, across, halves,
    hidden, gain, w_kv, lengths, table, freq,
    out,
    h_own, h_peer, w_buf, buf, id_row, table_all, table_s,
    h_sem, hs_sem, hr_sem, w_sem, ms_sem, mr_sem, t_sem,
    us_sem, ur_sem, ds_sem, dr_sem, ys_sem, yr_sem,
):
    n = depth * across
    seqs, rows, local = h_own.shape
    piece = w_buf.shape[1]
    per_half = PIECES // 2
    full = 2 * local
    me = lax.axis_index("seq")
    side = lax.axis_index("tensor")
    z = me // across
    y = me % across
    y_peer = z * across + (across - 1 - y)

    own_copies = [pltpu.make_async_copy(hidden.at[s], h_own.at[s], h_sem.at[s]) for s in range(seqs)]

    def w_copy(slot):
        half = side if slot < per_half else 1 - side
        index = half * per_half + slot % per_half
        return pltpu.make_async_copy(
            w_kv.at[pl.ds(index * piece, piece), :], w_buf.at[slot], w_sem.at[slot]
        )

    w_copies = [w_copy(i) for i in range(PIECES)]
    own_copies[0].start()
    for c in w_copies[:per_half]:
        c.start()

    id_lane = lax.broadcasted_iota(jnp.int32, (1, HD), 1)
    ids = jnp.full((1, HD), -1, jnp.int32)
    for s in range(seqs):
        ids = jnp.where(id_lane == s, table[s], ids)
    id_row[...] = ids

    barrier = pltpu.get_barrier_semaphore()
    pl.semaphore_signal(barrier, inc=1, device_id={"tensor": 1 - side}, device_id_type=MESH)
    for step in range(1, n):
        pl.semaphore_signal(
            barrier, inc=1, device_id={"seq": lax.rem(me + step, n)}, device_id_type=MESH
        )
    pl.semaphore_wait(barrier, n)

    def peer_copy(s, part):
        cut = pl.ds(part * piece, piece)
        i = s * per_half + part
        return pltpu.make_async_remote_copy(
            src_ref=hidden.at[s, :, cut], dst_ref=h_peer.at[s, :, cut],
            send_sem=hs_sem.at[i], recv_sem=hr_sem.at[i],
            device_id={"tensor": 1 - side}, device_id_type=MESH,
        )

    peer_copies = [[peer_copy(s, part) for part in range(per_half)] for s in range(seqs)]
    for c in peer_copies[0]:
        c.start()
    for c in w_copies[per_half:]:
        c.start()
    for s in range(1, seqs):
        own_copies[s].start()
        for c in peer_copies[s]:
            c.start()

    def id_copy(step):
        return pltpu.make_async_remote_copy(
            src_ref=id_row, dst_ref=table_all.at[me],
            send_sem=ms_sem.at[step - 1], recv_sem=mr_sem.at[step - 1],
            device_id={"seq": lax.rem(me + step, n)}, device_id_type=MESH,
        )

    def id_landed(step):
        return pltpu.make_async_remote_copy(
            src_ref=id_row, dst_ref=table_all.at[lax.rem(me + n - step, n)],
            send_sem=ms_sem.at[step - 1], recv_sem=mr_sem.at[step - 1],
            device_id={"seq": lax.rem(me + step, n)}, device_id_type=MESH,
        )

    for step in range(1, n):
        id_copy(step).start()
    table_all[me] = ids

    position = me * rows + lax.broadcasted_iota(jnp.int32, (rows, 1), 0)
    angle = position.astype(jnp.float32) * freq[...]
    cosine = jnp.cos(angle)
    lane = lax.broadcasted_iota(jnp.int32, (rows, HD), 1)
    sine = jnp.where(lane < HD // 2, -1.0, 1.0) * jnp.sin(angle)

    count = seqs * halves if halves else 1
    extra = 1 if across == 2 else 0
    stride = count + extra

    def unit(dev, u):
        if not halves:
            return buf.at[dev]
        part = rows // halves
        return buf.at[dev, u // halves, pl.ds((u % halves) * part, part), :]

    def send(ref, ssem, rsem, dev):
        return pltpu.make_async_remote_copy(
            src_ref=ref, dst_ref=ref, send_sem=ssem, recv_sem=rsem,
            device_id={"seq": dev}, device_id_type=MESH,
        )

    def up_send(k, u):
        ref = unit(me - k * across, u) if u < count else unit(y_peer - k * across, 0)
        i = k * stride + u
        return send(ref, us_sem.at[i], ur_sem.at[i], me + across)

    def down_send(k, u):
        ref = unit(me + k * across, u) if u < count else unit(y_peer + k * across, 0)
        i = k * stride + u
        return send(ref, ds_sem.at[i], dr_sem.at[i], me - across)

    def up_recv(k, u):
        far = (k + 1) * across
        ref = unit(me - far, u) if u < count else unit(y_peer - far, 0)
        i = k * stride + u
        return send(ref, us_sem.at[i], ur_sem.at[i], me - across)

    def down_recv(k, u):
        far = (k + 1) * across
        ref = unit(me + far, u) if u < count else unit(y_peer + far, 0)
        i = k * stride + u
        return send(ref, ds_sem.at[i], dr_sem.at[i], me + across)

    def side_copy(shift, u, base, mine):
        i = base + u
        ref = unit((me if mine else y_peer) + shift * across, u)
        return send(ref, ys_sem.at[i], yr_sem.at[i], y_peer)

    def up_base(k):
        return count * (1 + k)

    def down_base(k):
        return count * (depth + k)

    has_up = z + 1 < depth
    has_down = z >= 1

    def send_own(u):
        @pl.when(has_up)
        def _():
            up_send(0, u).start()

        @pl.when(has_down)
        def _():
            down_send(0, u).start()

        if across == 2:
            side_copy(0, u, 0, True).start()

    def project(first, many):
        size = many * rows
        acc = jnp.zeros((size, w_buf.shape[2]), jnp.float32)
        squares = jnp.zeros((size, HD), jnp.float32)
        for s in range(first, first + many):
            own_copies[s].wait()
        for slot in range(PIECES):
            if slot >= per_half:
                for s in range(first, first + many):
                    peer_copies[s][slot - per_half].wait_recv()
            if first == 0:
                w_copies[slot].wait()
            src = h_own if slot < per_half else h_peer
            half = side if slot < per_half else 1 - side
            at = (slot % per_half) * piece
            raw = src[pl.ds(first, many), :, pl.ds(at, piece)].reshape(size, piece)
            wide = raw.astype(jnp.float32)
            sq = wide * wide
            for j in range(piece // HD):
                squares = squares + sq[:, j * HD:(j + 1) * HD]
            scaled = (wide * gain[pl.ds(half * local + at, piece)].astype(jnp.float32).reshape(1, piece)).astype(jnp.bfloat16)
            acc = acc + jnp.dot(scaled, w_buf[slot], preferred_element_type=jnp.float32)
        total = jnp.sum(squares, axis=1, keepdims=True)
        acc = acc * lax.rsqrt(total / full + epsilon)
        for i in range(many):
            s = first + i
            living = position < lengths[s]
            for col in range(0, acc.shape[1], 2 * HD):
                key = acc[i * rows:(i + 1) * rows, col:col + HD]
                value = acc[i * rows:(i + 1) * rows, col + HD:col + 2 * HD]
                turned = key * cosine + pltpu.roll(key, HD // 2, 1) * sine
                buf[me, s, :, col:col + HD] = jnp.where(living, turned, 0.0).astype(jnp.bfloat16)
                buf[me, s, :, col + HD:col + 2 * HD] = jnp.where(living, value, 0.0).astype(jnp.bfloat16)

    project(0, 1)
    if halves:
        for u in range(halves):
            send_own(u)
    for s in range(1, seqs):
        project(s, 1)
        for u in range(s * halves, (s + 1) * halves):
            send_own(u)
    if not halves:
        send_own(0)

    if extra:
        side_copy(0, 0, 0, False).wait_recv()

        @pl.when(has_up)
        def _():
            up_send(0, count).start()

        @pl.when(has_down)
        def _():
            down_send(0, count).start()

    for step in range(1, n):
        id_landed(step).wait_recv()
    to_scalar = pltpu.make_async_copy(table_all, table_s, t_sem)
    to_scalar.start()
    to_scalar.wait()

    def look(dev, found):
        for s in range(seqs):
            page = table_s[dev, 0, s]
            found = tuple(
                jnp.where(page == me * SLOTS + j, dev * seqs + s, f) for j, f in enumerate(found)
            )
        return found

    found = lax.fori_loop(0, n, look, (jnp.int32(-1),) * SLOTS)

    for k in range(depth - 1):
        for u in range(stride):
            sideways = across == 2 and 0 < u < count

            @pl.when(z - 1 - k >= 0)
            def _():
                up_recv(k, u).wait_recv()
                if k + 1 < depth - 1:
                    @pl.when(has_up)
                    def _():
                        up_send(k + 1, u).start()
                if sideways:
                    side_copy(-(k + 1), u, up_base(k), True).start()

            @pl.when(z + 1 + k < depth)
            def _():
                down_recv(k, u).wait_recv()
                if k + 1 < depth - 1:
                    @pl.when(has_down)
                    def _():
                        down_send(k + 1, u).start()
                if sideways:
                    side_copy(k + 1, u, down_base(k), True).start()

    if across == 2:
        for u in range(1, count):
            side_copy(0, u, 0, False).wait_recv()
        for k in range(depth - 1):
            for u in range(1, count):
                @pl.when(z - 1 - k >= 0)
                def _():
                    side_copy(-(k + 1), u, up_base(k), False).wait_recv()

                @pl.when(z + 1 + k < depth)
                def _():
                    side_copy(k + 1, u, down_base(k), False).wait_recv()

    for j in range(SLOTS):
        index = jnp.maximum(found[j], 0)
        rows_j = buf[index // seqs, index % seqs]
        out[j] = jnp.where(found[j] >= 0, rows_j, jnp.zeros_like(rows_j))

    for s in range(seqs):
        for c in peer_copies[s]:
            c.wait_send()
    for step in range(1, n):
        id_copy(step).wait_send()
    for k in range(depth - 1):
        for u in range(stride):
            @pl.when(has_up & (z - k >= 0))
            def _():
                up_send(k, u).wait_send()

            @pl.when(has_down & (z + k < depth))
            def _():
                down_send(k, u).wait_send()
    if across == 2:
        for u in range(count):
            side_copy(0, u, 0, True).wait_send()
        for k in range(depth - 1):
            for u in range(1, count):
                @pl.when(z - 1 - k >= 0)
                def _():
                    side_copy(-(k + 1), u, up_base(k), True).wait_send()

                @pl.when(z + 1 + k < depth)
                def _():
                    side_copy(k + 1, u, down_base(k), True).wait_send()


def solution(mesh):
    n = mesh.shape["seq"]
    across = 2 if mesh.shape["group"] * 2 == PLANE and n % 2 == 0 else 1
    depth = n // across
    halves = 2 if across == 2 else 0

    def per_device(hidden, norm_gain, w_kv, lengths, page_table):
        seqs, rows, local = hidden.shape
        full, width = w_kv.shape
        assert rows == BLOCK and page_table.shape == (seqs, 1)
        piece = full // PIECES
        half_dim = HD // 2
        inv_freq = np.power(np.float64(rope_base), -2.0 * np.arange(half_dim) / HD)
        freq = jnp.asarray(np.tile(inv_freq, 2)[None, :].astype(np.float32))
        count = seqs * halves if halves else 1
        stride = count + (1 if across == 2 else 0)
        z_sems = pltpu.SemaphoreType.DMA((max(1, (depth - 1) * stride),))
        y_sems = pltpu.SemaphoreType.DMA((count * (2 * depth - 1) if across == 2 else 1,))
        vmem = pl.BlockSpec(memory_space=pltpu.VMEM)
        hbm = pl.BlockSpec(memory_space=pltpu.HBM)
        smem = pl.BlockSpec(memory_space=pltpu.SMEM)
        return pl.pallas_call(
            functools.partial(kernel, depth, across, halves),
            out_shape=jax.ShapeDtypeStruct((SLOTS, BLOCK, width), jnp.bfloat16),
            in_specs=[hbm, vmem, hbm, smem, smem, vmem],
            out_specs=vmem,
            scratch_shapes=[
                pltpu.VMEM((seqs, rows, local), jnp.bfloat16),
                pltpu.VMEM((seqs, rows, local), jnp.bfloat16),
                pltpu.VMEM((PIECES, piece, width), jnp.bfloat16),
                pltpu.VMEM((n, seqs, rows, width), jnp.bfloat16),
                pltpu.VMEM((1, HD), jnp.int32),
                pltpu.VMEM((n, 1, HD), jnp.int32),
                pltpu.SMEM((n, 1, HD), jnp.int32),
                pltpu.SemaphoreType.DMA((seqs,)),
                pltpu.SemaphoreType.DMA((seqs * PIECES // 2,)),
                pltpu.SemaphoreType.DMA((seqs * PIECES // 2,)),
                pltpu.SemaphoreType.DMA((PIECES,)),
                pltpu.SemaphoreType.DMA((n - 1,)),
                pltpu.SemaphoreType.DMA((n - 1,)),
                pltpu.SemaphoreType.DMA,
                z_sems, z_sems, z_sems, z_sems, y_sems, y_sems,
            ],
            compiler_params=pltpu.CompilerParams(collective_id=0, has_side_effects=True, vmem_limit_bytes=63 * 1000 * 1024),
        )(hidden, norm_gain, w_kv, lengths, page_table.reshape(seqs), freq)

    return jax.shard_map(
        per_device,
        mesh=mesh,
        in_specs=(P("group", "seq", "tensor"), P(), P(None, "tensor"), P("group"), P("group", "seq")),
        out_specs=P(("group", "seq"), None, "tensor"),
        check_vma=False,
    )
```

profile of v0, /device:TPU:0, one launch (start us, length us, event | category | flops | bytes accessed | tf_op | source)
XLA Modules:
  0.0 48.0 jit_solution(16422676134357585429)
XLA Ops:
  0.0 45.7 %shard_map.64 = bf16[8,128,512]{2,1,0:T(8,128)(2,1)} custom-call(bf16[3,128,4096]{2,1,0:T(8,128)(2,1)} %hidden.1, bf16[8192]{0:T(1024)(128)(2,1)} %gain.1, bf16[8192,512]{1,0:T(8,128)(2,1)} %w_kv.1, s32[3]{0:T(128)} %lengths.1, s32[3]{0:T(128)} %bitcast.1, f32[1,128]{1,0:T(1,128)} %constant.2.clone.freq), custom_call_target="tpu_custom_call" | custom-call | tf_op jit(solution)/shard_map/pallas_call | solution.py:339
  45.7 2.3 %copy.8 = bf16[8,128,512]{2,1,0:T(8,128)(2,1)} copy(bf16[8,128,512]{2,1,0:T(8,128)(2,1)} %shard_map.64) | data formatting | bytes 2097152
where the time goes:
time: 48.2 us; the launch traced here: 48 us
  Pallas kernels  45.7 us (95%)
  local copies, waits for them, and re-layouts  2.26 us (5%)
    pallas_call x1, Pallas kernels, per_device(): pl.pallas_call(functools.partial(kernel, depth, across, halves), out_shap...  45.7 us
    unnamed x1, local copies, waits for them, and re-layouts  2.26 us

commit v1 on v0

--- a/solution.py
+++ b/solution.py
@@ -338,7 +338,7 @@
         smem = pl.BlockSpec(memory_space=pltpu.SMEM)
         return pl.pallas_call(
             functools.partial(kernel, depth, across, halves),
-            out_shape=jax.ShapeDtypeStruct((SLOTS, BLOCK, width), jnp.bfloat16),
+            out_shape=pltpu.VMEM((SLOTS, BLOCK, width), jnp.bfloat16),
             in_specs=[hbm, vmem, hbm, smem, smem, vmem],
             out_specs=vmem,
             scratch_shapes=[

time: 48.2 us -> 46 us (0.954)
  local copies, waits for them, and re-layouts: 2.26 us -> 0.97 us
  Pallas kernels: 45.7 us -> 44.8 us
    unnamed x1, local copies, waits for them, and re-layouts: 2.26 us -> 0.97 us
    pallas_call x1, Pallas kernels: 45.7 us -> 44.8 us  [per_device(): pl.pallas_call(functools.partial(kernel, depth, across, halves), out_shap...]
where the time goes in v1:
time: 46 us; the launch traced here: 45.8 us
  Pallas kernels  44.8 us (97%)
  local copies, waits for them, and re-layouts  0.97 us (2%)
    pallas_call x1, Pallas kernels, per_device(): pl.pallas_call(functools.partial(kernel, depth, across, halves), out_shap...  44.8 us
    unnamed x1, local copies, waits for them, and re-layouts  0.97 us

profile of v1, /device:TPU:0, one launch (start us, length us, event | category | flops | bytes accessed | tf_op | source)
XLA Modules:
  0.0 45.8 jit_solution(15849159628399609035)
XLA Ops:
  0.0 44.8 %shard_map.64 = bf16[8,128,512]{2,1,0:T(8,128)(2,1)S(1)} custom-call(bf16[3,128,4096]{2,1,0:T(8,128)(2,1)} %hidden.1, bf16[8192]{0:T(1024)(128)(2,1)} %gain.1, bf16[8192,512]{1,0:T(8,128)(2,1)} %w_kv.1, s32[3]{0:T(128)} %lengths.1, s32[3]{0:T(128)} %bitcast.1, f32[1,128]{1,0:T(1,128)} %constant.2.clone.freq), custom_call_target="tpu_custom_call" | custom-call | tf_op jit(solution)/shard_map/pallas_call | solution.py:339
  44.8 1.0 %copy.8 = bf16[8,128,512]{2,1,0:T(8,128)(2,1)} copy(bf16[8,128,512]{2,1,0:T(8,128)(2,1)S(1)} %shard_map.64) | data formatting | bytes 2097152

commit v2 on v1

v2 whole, which is shorter than its diff:
```python
import functools

import jax
import jax.numpy as jnp
import numpy as np
from jax import lax
from jax.experimental import pallas as pl
from jax.experimental.pallas import tpu as pltpu
from jax.sharding import PartitionSpec as P

HD = 128
BLOCK = 128
SLOTS = 8
PIECES = 8
PLANE = 4

epsilon = 1e-05
rope_base = 500000.0
MESH = pl.DeviceIdType.MESH


def kernel(
    depth, across, slots,
    hidden, gain_hbm, w_kv, lengths_hbm, table_hbm, freq_hbm,
    out,
    h_own, h_peer, w_buf, buf, cross, gain, freq, lengths, table, table_all, table_s,
    h_sem, hs_sem, hr_sem, w_sem, in_sem, is_sem, ir_sem, t_sem,
    us_sem, ur_sem, ds_sem, dr_sem, ys_sem, yr_sem,
):
    n = depth * across
    seqs, rows, local = h_own.shape
    piece = w_buf.shape[1]
    per_half = PIECES // 2
    full = 2 * local
    me = lax.axis_index("seq")
    side = lax.axis_index("tensor")
    z = me // across
    y = me % across
    y_peer = z * across + (across - 1 - y)
    has_up = z + 1 < depth
    has_down = z >= 1
    pair = across == 2

    own_copies = [pltpu.make_async_copy(hidden.at[s], h_own.at[s], h_sem.at[s]) for s in range(seqs)]

    def w_copy(slot):
        half = side if slot < per_half else 1 - side
        index = half * per_half + slot % per_half
        return pltpu.make_async_copy(
            w_kv.at[pl.ds(index * piece, piece), :], w_buf.at[slot], w_sem.at[slot]
        )

    w_copies = [w_copy(i) for i in range(PIECES)]
    own_copies[0].start()
    for c in w_copies[:per_half]:
        c.start()
    smalls = [
        pltpu.make_async_copy(src, dst, in_sem.at[i])
        for i, (src, dst) in enumerate(
            [(table_hbm, table), (freq_hbm, freq), (gain_hbm, gain), (lengths_hbm, lengths)]
        )
    ]
    for c in smalls:
        c.start()

    barrier = pltpu.get_barrier_semaphore()

    def greet(device):
        pl.semaphore_signal(barrier, inc=1, device_id=device, device_id_type=MESH)

    greet({"tensor": 1 - side})
    if pair:
        greet({"seq": y_peer})

    @pl.when(has_up)
    def _():
        greet({"seq": me + across})

    @pl.when(has_down)
    def _():
        greet({"seq": me - across})

    pl.semaphore_wait(barrier, across + has_up.astype(jnp.int32) + has_down.astype(jnp.int32))

    def peer_copy(s, part):
        cut = pl.ds(part * piece, piece)
        i = s * per_half + part
        return pltpu.make_async_remote_copy(
            src_ref=hidden.at[s, :, cut], dst_ref=h_peer.at[s, :, cut],
            send_sem=hs_sem.at[i], recv_sem=hr_sem.at[i],
            device_id={"tensor": 1 - side}, device_id_type=MESH,
        )

    peer_copies = [[peer_copy(s, part) for part in range(per_half)] for s in range(seqs)]
    for c in peer_copies[0]:
        c.start()
    for c in w_copies[per_half:]:
        c.start()
    for s in range(1, seqs):
        own_copies[s].start()
        for c in peer_copies[s]:
            c.start()

    smalls[0].wait()
    id_lane = lax.broadcasted_iota(jnp.int32, (1, HD), 1)
    ids = jnp.full((1, HD), -1, jnp.int32)
    for s in range(seqs):
        ids = jnp.where(id_lane == s, table[s], ids)
    table_all[y, z] = ids
    smalls[1].wait()
    position = me * rows + lax.broadcasted_iota(jnp.int32, (rows, 1), 0)
    angle = position.astype(jnp.float32) * freq[...]
    cosine = jnp.cos(angle)
    lane = lax.broadcasted_iota(jnp.int32, (rows, HD), 1)
    sine = jnp.where(lane < HD // 2, -1.0, 1.0) * jnp.sin(angle)

    def send(src, dst, ssem, rsem, dev):
        return pltpu.make_async_remote_copy(
            src_ref=src, dst_ref=dst, send_sem=ssem, recv_sem=rsem,
            device_id={"seq": dev}, device_id_type=MESH,
        )

    part = rows // 2
    tail = (seqs - 1, 0)
    if pair:
        units = [(s, h) for s in range(seqs) for h in range(2) if (s, h) != tail] + [tail]
    else:
        units = [None]
    stride = len(units) + 1

    def half(block, h):
        return buf.at[block, pl.ds(h * part, part), :]

    def own_unit(dev, i):
        if not pair:
            return buf.at[pl.ds(dev * seqs, seqs)]
        return half(dev * seqs + units[i][0], units[i][1])

    def extra_unit(zz):
        return half((zz * across + across - 1 - y) * seqs + tail[0], tail[1])

    def up(ref, k, i, dev):
        return send(ref, ref, us_sem.at[k * stride + i], ur_sem.at[k * stride + i], dev)

    def down(ref, k, i, dev):
        return send(ref, ref, ds_sem.at[k * stride + i], dr_sem.at[k * stride + i], dev)

    def id_up(zz, k, dev):
        ref = table_all.at[y, zz]
        return send(ref, ref, is_sem.at[k], ir_sem.at[k], dev)

    def id_down(zz, k, dev):
        ref = table_all.at[y, zz]
        return send(ref, ref, is_sem.at[depth + k], ir_sem.at[depth + k], dev)

    def id_side(yy):
        ref = table_all.at[yy]
        return send(ref, ref, is_sem.at[2 * depth], ir_sem.at[2 * depth], y_peer)

    def tail_side(dev):
        ref = half(dev * seqs + tail[0], tail[1])
        return send(ref, ref, ys_sem.at[2 * slots], yr_sem.at[2 * slots], y_peer)

    def cross_send(j, h):
        cut = pl.ds(h * part, part)
        return send(
            cross.at[j, cut, :], buf.at[n * seqs + j, cut, :],
            ys_sem.at[2 * j + h], yr_sem.at[2 * j + h], y_peer,
        )

    def id_scalar(yy, zz, i):
        return pltpu.make_async_copy(table_all.at[yy, zz], table_s.at[yy, zz], t_sem.at[i])

    def send_own(i):
        @pl.when(has_down)
        def _():
            down(own_unit(me, i), 0, i, me - across).start()

        @pl.when(has_up)
        def _():
            up(own_unit(me, i), 0, i, me + across).start()

    def send_ids():
        @pl.when(has_down)
        def _():
            id_down(z, 0, me - across).start()

        @pl.when(has_up)
        def _():
            id_up(z, 0, me + across).start()

    def project(s):
        acc = jnp.zeros((rows, w_buf.shape[2]), jnp.float32)
        squares = jnp.zeros((rows, HD), jnp.float32)
        own_copies[s].wait()
        for slot in range(PIECES):
            if slot >= per_half:
                peer_copies[s][slot - per_half].wait_recv()
            if s == 0:
                w_copies[slot].wait()
            src = h_own if slot < per_half else h_peer
            half_of = side if slot < per_half else 1 - side
            at = (slot % per_half) * piece
            raw = src[s, :, pl.ds(at, piece)]
            wide = raw.astype(jnp.float32)
            sq = wide * wide
            for j in range(piece // HD):
                squares = squares + sq[:, j * HD:(j + 1) * HD]
            scaled = (wide * gain[pl.ds(half_of * local + at, piece)].astype(jnp.float32).reshape(1, piece)).astype(jnp.bfloat16)
            acc = acc + jnp.dot(scaled, w_buf[slot], preferred_element_type=jnp.float32)
        total = jnp.sum(squares, axis=1, keepdims=True)
        acc = acc * lax.rsqrt(total / full + epsilon)
        living = position < lengths[s]
        for col in range(0, acc.shape[1], 2 * HD):
            key = acc[:, col:col + HD]
            value = acc[:, col + HD:col + 2 * HD]
            turned = key * cosine + pltpu.roll(key, HD // 2, 1) * sine
            buf[me * seqs + s, :, col:col + HD] = jnp.where(living, turned, 0.0).astype(jnp.bfloat16)
            buf[me * seqs + s, :, col + HD:col + 2 * HD] = jnp.where(living, value, 0.0).astype(jnp.bfloat16)

    smalls[2].wait()
    smalls[3].wait()
    at_edge = (z == 0) | (z == depth - 1)
    for s in range(seqs):
        project(s)
        if s == 0:
            send_ids()
        if pair:
            if s == tail[0]:
                @pl.when(at_edge)
                def _():
                    tail_side(me).start()
            for i, (us, _) in enumerate(units):
                if us == s:
                    send_own(i)
    if not pair:
        send_own(0)
    own_scalar = id_scalar(y, z, 2 * depth)
    own_scalar.start()

    if pair:
        @pl.when(at_edge)
        def _():
            tail_side(y_peer).wait_recv()

        @pl.when(z == 0)
        def _():
            up(extra_unit(0), 0, stride - 1, me + across).start()

        @pl.when(z == depth - 1)
        def _():
            down(extra_unit(depth - 1), 0, stride - 1, me - across).start()

    own_scalar.wait()

    if not pair:
        for k in range(depth - 1):
            @pl.when(z - 1 - k >= 0)
            def _():
                id_up(z - 1 - k, k, me - across).wait_recv()
                if k + 1 < depth - 1:
                    @pl.when(has_up)
                    def _():
                        id_up(z - 1 - k, k + 1, me + across).start()
                up(own_unit(me - (k + 1), 0), k, 0, me - across).wait_recv()
                if k + 1 < depth - 1:
                    @pl.when(has_up)
                    def _():
                        up(own_unit(me - (k + 1), 0), k + 1, 0, me + across).start()

            @pl.when(z + 1 + k < depth)
            def _():
                id_down(z + 1 + k, k, me + across).wait_recv()
                if k + 1 < depth - 1:
                    @pl.when(has_down)
                    def _():
                        id_down(z + 1 + k, k + 1, me - across).start()
                down(own_unit(me + (k + 1), 0), k, 0, me + across).wait_recv()
                if k + 1 < depth - 1:
                    @pl.when(has_down)
                    def _():
                        down(own_unit(me + (k + 1), 0), k + 1, 0, me - across).start()

        to_scalar = pltpu.make_async_copy(table_all, table_s, t_sem.at[0])
        to_scalar.start()
        to_scalar.wait()

        def look(dev, found):
            for s in range(seqs):
                page = table_s[0, dev, 0, s]
                found = tuple(
                    jnp.where(page == me * SLOTS + j, dev * seqs + s, f) for j, f in enumerate(found)
                )
            return found

        found = lax.fori_loop(0, n, look, (jnp.int32(-1),) * SLOTS)
        where_is = [found, found]
    else:
        total = seqs * depth
        near = jnp.minimum(z, depth - 1 - z)
        below_far = z > depth - 1 - z
        first_pop = [total - 1 - slots, total - slots]

        def arrival(a):
            if a < seqs:
                return z, jnp.int32(a), z >= depth, jnp.int32(0)
            i = a - seqs
            both = i < near * 2 * seqs
            rest = i - near * 2 * seqs
            k = jnp.where(both, i // (2 * seqs), near + rest // seqs)
            s = jnp.where(both, (i % (2 * seqs)) // 2, rest % seqs)
            below = (both & (i % 2 == 0)) | (jnp.logical_not(both) & below_far)
            zz = jnp.where(below, z - 1 - k, z + 1 + k)
            return zz, s, below, k

        arrivals = [arrival(a) for a in range(total)]

        def is_tail(a):
            zz, s, _, _ = arrivals[a]
            return ((zz == 0) | (zz == depth - 1)) & (s == tail[0])

        def queue(lane_of, a, target, last, places):
            zz, s, _, _ = arrivals[a]
            page = table_s[lane_of, zz, 0, s]
            wanted = (page >= target * SLOTS) & (page < target * SLOTS + SLOTS)
            for h in range(2):
                goes = wanted & jnp.logical_not(is_tail(a)) if h == tail[1] else wanted
                place = jnp.maximum(last[h] + 1, max(a - first_pop[h], 0))
                places[h].append(jnp.where(goes, place, -1))
                last[h] = jnp.where(goes, place, last[h])

        def pop(h, a, places):
            j = a - first_pop[h]
            if j < 0 or j >= slots:
                return
            cut = pl.ds(h * part, part)
            content = None
            for c in range(j, a + 1):
                zz, s, _, _ = arrivals[c]
                rows_c = buf[(zz * across + y) * seqs + s, cut, :]
                content = rows_c if content is None else jnp.where(places[h][c] == j, rows_c, content)
            cross[j, cut, :] = content
            cross_send(j, h).start()

        def relay(a, h):
            zz, s, below, k = arrivals[a]
            ref = half((zz * across + y) * seqs + s, h)
            last_s = s == tail[0]
            i = jnp.where(last_s, 2 * seqs - 1 if h == tail[1] else 2 * seqs - 2, 2 * s + h)

            @pl.when(below)
            def _():
                up(ref, k, i, me - across).wait_recv()

                @pl.when(has_up)
                def _():
                    up(ref, k + 1, i, me + across).start()

            @pl.when(jnp.logical_not(below))
            def _():
                down(ref, k, i, me + across).wait_recv()

                @pl.when(has_down)
                def _():
                    down(ref, k + 1, i, me - across).start()

        def relay_id(a):
            zz, s, below, k = arrivals[a]

            @pl.when(below & (s == 0))
            def _():
                id_up(zz, k, me - across).wait_recv()

                @pl.when(has_up)
                def _():
                    id_up(zz, k + 1, me + across).start()

            @pl.when(jnp.logical_not(below) & (s == 0))
            def _():
                id_down(zz, k, me + across).wait_recv()

                @pl.when(has_down)
                def _():
                    id_down(zz, k + 1, me - across).start()

            @pl.when(s == 0)
            def _():
                id_scalar(y, zz, zz).start()

        def relay_extra(a):
            zz, s, below, k = arrivals[a]

            @pl.when(is_tail(a) & below)
            def _():
                up(extra_unit(zz), k, stride - 1, me - across).wait_recv()

                @pl.when(has_up)
                def _():
                    up(extra_unit(zz), k + 1, stride - 1, me + across).start()

            @pl.when(is_tail(a) & jnp.logical_not(below))
            def _():
                down(extra_unit(zz), k, stride - 1, me + across).wait_recv()

                @pl.when(has_down)
                def _():
                    down(extra_unit(zz), k + 1, stride - 1, me - across).start()

        last = [jnp.int32(-1), jnp.int32(-1)]
        places = [[], []]
        for a in range(seqs):
            queue(y, a, y_peer, last, places)
        for a in range(seqs, total):
            zz, s, _, _ = arrivals[a]
            relay_id(a)
            order = (1 - tail[1], tail[1]) if a == total - 1 else (0, 1)
            relay(a, order[0])

            @pl.when(s == 0)
            def _():
                id_scalar(y, zz, zz).wait()

            queue(y, a, y_peer, last, places)
            if a == total - seqs:
                id_side(y).start()
            if a == total - 2:
                pop(order[0], a, places)
                relay(a, order[1])
                pop(order[1], a, places)
                relay_extra(a)
                id_side(1 - y).wait_recv()
                rest = pltpu.make_async_copy(table_all.at[1 - y], table_s.at[1 - y], t_sem.at[2 * depth + 1])
                rest.start()
                rest.wait()
                continue
            if a == total - 1:
                found = [[jnp.int32(-1)] * SLOTS for _ in range(2)]
                peer_last = [jnp.int32(-1), jnp.int32(-1)]
                peer_places = [[], []]
                for c in range(total):
                    cz, cs, _, _ = arrivals[c]
                    queue(1 - y, c, me, peer_last, peer_places)
                    mine = table_s[y, cz, 0, cs] - me * SLOTS
                    theirs = table_s[1 - y, cz, 0, cs] - me * SLOTS
                    here = (cz * across + y) * seqs + cs
                    there = (cz * across + 1 - y) * seqs + cs
                    for h in range(2):
                        place = n * seqs + peer_places[h][c]
                        if h == tail[1]:
                            place = jnp.where(is_tail(c), there, place)
                        found[h] = [
                            jnp.where(mine == j, here, jnp.where(theirs == j, place, f))
                            for j, f in enumerate(found[h])
                        ]
                where_is = found
            pop(order[0], a, places)
            relay(a, order[1])
            pop(order[1], a, places)
            relay_extra(a)
        for j in range(slots):
            for h in range(2):
                cross_send(j, h).wait_recv()

    for h in range(2):
        cut = pl.ds(h * part, part)
        for j in range(SLOTS):
            index = where_is[h][j]
            rows_j = buf[jnp.maximum(index, 0), cut, :]
            out[j, cut, :] = jnp.where(index >= 0, rows_j, jnp.zeros_like(rows_j))

    for s in range(seqs):
        for c in peer_copies[s]:
            c.wait_send()
    for k in range(depth - 1):
        @pl.when(has_up & (z - k >= 0))
        def _():
            id_up(z - k, k, me + across).wait_send()
            for i in range(len(units)):
                up(own_unit(me - k * across, i), k, i, me + across).wait_send()

        @pl.when(has_down & (z + k < depth))
        def _():
            id_down(z + k, k, me - across).wait_send()
            for i in range(len(units)):
                down(own_unit(me + k * across, i), k, i, me - across).wait_send()
    if pair:
        @pl.when(has_up)
        def _():
            up(extra_unit(0), z, stride - 1, me + across).wait_send()

        @pl.when(has_down)
        def _():
            down(extra_unit(depth - 1), depth - 1 - z, stride - 1, me - across).wait_send()

        @pl.when(at_edge)
        def _():
            tail_side(me).wait_send()

        id_side(y).wait_send()
        for j in range(slots):
            for h in range(2):
                cross_send(j, h).wait_send()


def solution(mesh):
    n = mesh.shape["seq"]

    def per_device(hidden, norm_gain, w_kv, lengths, page_table):
        seqs, rows, local = hidden.shape
        full, width = w_kv.shape
        assert rows == BLOCK and page_table.shape == (seqs, 1)
        wide = mesh.shape["group"] * 2 == PLANE and n % 2 == 0 and seqs * (n // 2) > SLOTS
        across = 2 if wide else 1
        depth = n // across
        slots = SLOTS if wide else 0
        piece = full // PIECES
        half_dim = HD // 2
        inv_freq = np.power(np.float64(rope_base), -2.0 * np.arange(half_dim) / HD)
        freq = jnp.asarray(np.tile(inv_freq, 2)[None, :].astype(np.float32))
        stride = (2 * seqs if wide else 1) + 1
        z_sems = pltpu.SemaphoreType.DMA((max(1, (depth - 1) * stride),))
        y_sems = pltpu.SemaphoreType.DMA((2 * slots + 1,))
        vmem = pl.BlockSpec(memory_space=pltpu.VMEM)
        hbm = pl.BlockSpec(memory_space=pltpu.HBM)
        return pl.pallas_call(
            functools.partial(kernel, depth, across, slots),
            out_shape=pltpu.VMEM((SLOTS, BLOCK, width), jnp.bfloat16),
            in_specs=[hbm] * 6,
            out_specs=vmem,
            scratch_shapes=[
                pltpu.VMEM((seqs, rows, local), jnp.bfloat16),
                pltpu.VMEM((seqs, rows, local), jnp.bfloat16),
                pltpu.VMEM((PIECES, piece, width), jnp.bfloat16),
                pltpu.VMEM((n * seqs + slots, rows, width), jnp.bfloat16),
                pltpu.VMEM((max(1, slots), rows, width), jnp.bfloat16),
                pltpu.VMEM((full,), jnp.bfloat16),
                pltpu.VMEM((1, HD), jnp.float32),
                pltpu.SMEM((seqs,), jnp.int32),
                pltpu.SMEM((seqs,), jnp.int32),
                pltpu.VMEM((across, depth, 1, HD), jnp.int32),
                pltpu.SMEM((across, depth, 1, HD), jnp.int32),
                pltpu.SemaphoreType.DMA((seqs,)),
                pltpu.SemaphoreType.DMA((seqs * PIECES // 2,)),
                pltpu.SemaphoreType.DMA((seqs * PIECES // 2,)),
                pltpu.SemaphoreType.DMA((PIECES,)),
                pltpu.SemaphoreType.DMA((4,)),
                pltpu.SemaphoreType.DMA((2 * depth + 1,)),
                pltpu.SemaphoreType.DMA((2 * depth + 1,)),
                pltpu.SemaphoreType.DMA((2 * depth + 2,)),
                z_sems, z_sems, z_sems, z_sems, y_sems, y_sems,
            ],
            compiler_params=pltpu.CompilerParams(collective_id=0, has_side_effects=True, vmem_limit_bytes=63 * 1000 * 1024),
        )(hidden, norm_gain, w_kv, lengths, page_table.reshape(seqs), freq)

    return jax.shard_map(
        per_device,
        mesh=mesh,
        in_specs=(P("group", "seq", "tensor"), P(), P(None, "tensor"), P("group"), P("group", "seq")),
        out_specs=P(("group", "seq"), None, "tensor"),
        check_vma=False,
    )
```

time: 46 us -> 41.1 us (0.89)
  Pallas kernels: 44.8 us -> 39.9 us
    pallas_call x1, Pallas kernels: 44.8 us -> 39.9 us  [per_device(): pl.pallas_call(functools.partial(kernel, depth, across, slots), out_shape...]
where the time goes in v2:
time: 41.1 us; the launch traced here: 40.9 us
  Pallas kernels  39.9 us (97%)
  local copies, waits for them, and re-layouts  0.97 us (2%)
    pallas_call x1, Pallas kernels, per_device(): pl.pallas_call(functools.partial(kernel, depth, across, slots), out_shape...  39.9 us
    unnamed x1, local copies, waits for them, and re-layouts  0.97 us

profile of v2, /device:TPU:0, one launch (start us, length us, event | category | flops | bytes accessed | tf_op | source)
XLA Modules:
  0.0 40.9 jit_solution(3165497713308438807)
XLA Ops:
  0.0 39.9 %shard_map.64 = bf16[8,128,512]{2,1,0:T(8,128)(2,1)S(1)} custom-call(bf16[3,128,4096]{2,1,0:T(8,128)(2,1)} %hidden.1, bf16[8192]{0:T(1024)(128)(2,1)} %gain_hbm.1, bf16[8192,512]{1,0:T(8,128)(2,1)} %w_kv.1, s32[3]{0:T(128)} %lengths_hbm.1, s32[3]{0:T(128)} %bitcast.1, f32[1,128]{1,0:T(1,128)} %constant.2.clone.freq_hbm), custom_call_target="tpu_custom_call" | custom-call | tf_op jit(solution)/shard_map/pallas_call | solution.py:525
  40.0 1.0 %copy.8 = bf16[8,128,512]{2,1,0:T(8,128)(2,1)} copy(bf16[8,128,512]{2,1,0:T(8,128)(2,1)S(1)} %shard_map.64) | data formatting | bytes 2097152

commit v3 on v2

--- a/solution.py
+++ b/solution.py
@@ -25,7 +25,7 @@
     out,
     h_own, h_peer, w_buf, buf, cross, gain, freq, lengths, table, table_all, table_s,
     h_sem, hs_sem, hr_sem, w_sem, in_sem, is_sem, ir_sem, t_sem,
-    us_sem, ur_sem, ds_sem, dr_sem, ys_sem, yr_sem,
+    us_sem, ur_sem, ds_sem, dr_sem, ys_sem, yr_sem, in_up, in_side,
 ):
     n = depth * across
     seqs, rows, local = h_own.shape
@@ -69,18 +69,19 @@
         pl.semaphore_signal(barrier, inc=1, device_id=device, device_id_type=MESH)
 
     greet({"tensor": 1 - side})
-    if pair:
-        greet({"seq": y_peer})
 
     @pl.when(has_up)
     def _():
         greet({"seq": me + across})
 
-    @pl.when(has_down)
-    def _():
-        greet({"seq": me - across})
-
-    pl.semaphore_wait(barrier, across + has_up.astype(jnp.int32) + has_down.astype(jnp.int32))
+    expected = 1 + has_down.astype(jnp.int32)
+    if pair:
+        @pl.when(y == 0)
+        def _():
+            greet({"seq": y_peer})
+
+        expected = expected + y
+    pl.semaphore_wait(barrier, expected)
 
     def peer_copy(s, part):
         cut = pl.ds(part * piece, piece)
@@ -100,6 +101,15 @@
         own_copies[s].start()
         for c in peer_copies[s]:
             c.start()
+
+    @pl.when(has_down)
+    def _():
+        pl.semaphore_signal(in_up, inc=1, device_id={"seq": me - across}, device_id_type=MESH)
+
+    if pair:
+        @pl.when(y == 1)
+        def _():
+            pl.semaphore_signal(in_side, inc=1, device_id={"seq": y_peer}, device_id_type=MESH)
 
     smalls[0].wait()
     id_lane = lax.broadcasted_iota(jnp.int32, (1, HD), 1)
@@ -121,23 +131,25 @@
         )
 
     part = rows // 2
-    tail = (seqs - 1, 0)
+    quarter = rows // 4
+    tail = seqs - 1
+    pieces = [(part, quarter), (part + quarter, quarter), (0, part)]
     if pair:
-        units = [(s, h) for s in range(seqs) for h in range(2) if (s, h) != tail] + [tail]
+        units = [(s, lo, part) for s in range(tail) for lo in (0, part)] + [(tail, lo, size) for lo, size in pieces]
     else:
         units = [None]
     stride = len(units) + 1
 
-    def half(block, h):
-        return buf.at[block, pl.ds(h * part, part), :]
+    def strip(block, lo, size):
+        return buf.at[block, pl.ds(lo, size), :]
 
     def own_unit(dev, i):
         if not pair:
             return buf.at[pl.ds(dev * seqs, seqs)]
-        return half(dev * seqs + units[i][0], units[i][1])
+        return strip(dev * seqs + units[i][0], units[i][1], units[i][2])
 
     def extra_unit(zz):
-        return half((zz * across + across - 1 - y) * seqs + tail[0], tail[1])
+        return strip((zz * across + across - 1 - y) * seqs + tail, 0, part)
 
     def up(ref, k, i, dev):
         return send(ref, ref, us_sem.at[k * stride + i], ur_sem.at[k * stride + i], dev)
@@ -158,15 +170,24 @@
         return send(ref, ref, is_sem.at[2 * depth], ir_sem.at[2 * depth], y_peer)
 
     def tail_side(dev):
-        ref = half(dev * seqs + tail[0], tail[1])
-        return send(ref, ref, ys_sem.at[2 * slots], yr_sem.at[2 * slots], y_peer)
-
-    def cross_send(j, h):
-        cut = pl.ds(h * part, part)
+        ref = strip(dev * seqs + tail, 0, part)
+        return send(ref, ref, ys_sem.at[3 * slots], yr_sem.at[3 * slots], y_peer)
+
+    def cross_pieces(h, j):
+        if h == 0:
+            return [(0, part)]
+        if j < slots - 1:
+            return [(part, part)]
+        return [(part, quarter), (part + quarter, quarter)]
+
+    def cross_send(j, lo, size):
+        i = 3 * j + (0 if lo == 0 else 1 if lo == part else 2)
+        cut = pl.ds(lo, size)
         return send(
-            cross.at[j, cut, :], buf.at[n * seqs + j, cut, :],
-            ys_sem.at[2 * j + h], yr_sem.at[2 * j + h], y_peer,
+            cross.at[j, cut, :], buf.at[n * seqs + j, cut, :], ys_sem.at[i], yr_sem.at[i], y_peer,
         )
+
+    all_cross = [(j, lo, size) for j in range(slots) for h in range(2) for lo, size in cross_pieces(h, j)]
 
     def id_scalar(yy, zz, i):
         return pltpu.make_async_copy(table_all.at[yy, zz], table_s.at[yy, zz], t_sem.at[i])
@@ -187,6 +208,7 @@
 
         @pl.when(has_up)
         def _():
+            pl.semaphore_wait(in_up, 1)
             id_up(z, 0, me + across).start()
 
     def project(s):
@@ -218,6 +240,20 @@
             buf[me * seqs + s, :, col:col + HD] = jnp.where(living, turned, 0.0).astype(jnp.bfloat16)
             buf[me * seqs + s, :, col + HD:col + 2 * HD] = jnp.where(living, value, 0.0).astype(jnp.bfloat16)
 
+    def settle(ks):
+        for k in ks:
+            @pl.when(has_up & (z - k >= 0))
+            def _():
+                id_up(z - k, k, me + across).wait_send()
+                for i in range(len(units)):
+                    up(own_unit(me - k * across, i), k, i, me + across).wait_send()
+
+            @pl.when(has_down & (z + k < depth))
+            def _():
+                id_down(z + k, k, me - across).wait_send()
+                for i in range(len(units)):
+                    down(own_unit(me + k * across, i), k, i, me - across).wait_send()
+
     smalls[2].wait()
     smalls[3].wait()
     at_edge = (z == 0) | (z == depth - 1)
@@ -226,15 +262,29 @@
         if s == 0:
             send_ids()
         if pair:
-            if s == tail[0]:
+            if s == tail:
+                @pl.when(y == 0)
+                def _():
+                    pl.semaphore_wait(in_side, 1)
+
                 @pl.when(at_edge)
                 def _():
                     tail_side(me).start()
-            for i, (us, _) in enumerate(units):
-                if us == s:
+            mine = [i for i, unit in enumerate(units) if unit[0] == s]
+            if s < tail:
+                for i in mine:
                     send_own(i)
+            else:
+                for when, order in ((at_edge, mine), (jnp.logical_not(at_edge), mine[-1:] + mine[:-1])):
+                    @pl.when(when)
+                    def _():
+                        for i in order:
+                            send_own(i)
     if not pair:
         send_own(0)
+    for s in range(seqs):
+        for c in peer_copies[s]:
+            c.wait_send()
     own_scalar = id_scalar(y, z, 2 * depth)
     own_scalar.start()
 
@@ -317,38 +367,37 @@
 
         def is_tail(a):
             zz, s, _, _ = arrivals[a]
-            return ((zz == 0) | (zz == depth - 1)) & (s == tail[0])
+            return ((zz == 0) | (zz == depth - 1)) & (s == tail)
 
         def queue(lane_of, a, target, last, places):
             zz, s, _, _ = arrivals[a]
             page = table_s[lane_of, zz, 0, s]
             wanted = (page >= target * SLOTS) & (page < target * SLOTS + SLOTS)
             for h in range(2):
-                goes = wanted & jnp.logical_not(is_tail(a)) if h == tail[1] else wanted
+                goes = wanted & jnp.logical_not(is_tail(a)) if h == 0 else wanted
                 place = jnp.maximum(last[h] + 1, max(a - first_pop[h], 0))
                 places[h].append(jnp.where(goes, place, -1))
                 last[h] = jnp.where(goes, place, last[h])
 
-        def pop(h, a, places):
+        def pop(h, a, places, cuts=None):
             j = a - first_pop[h]
             if j < 0 or j >= slots:
                 return
-            cut = pl.ds(h * part, part)
-            content = None
-            for c in range(j, a + 1):
-                zz, s, _, _ = arrivals[c]
-                rows_c = buf[(zz * across + y) * seqs + s, cut, :]
-                content = rows_c if content is None else jnp.where(places[h][c] == j, rows_c, content)
-            cross[j, cut, :] = content
-            cross_send(j, h).start()
-
-        def relay(a, h):
+            for lo, size in cuts or cross_pieces(h, j):
+                cut = pl.ds(lo, size)
+                content = None
+                for c in range(j, a + 1):
+                    zz, s, _, _ = arrivals[c]
+                    rows_c = buf[(zz * across + y) * seqs + s, cut, :]
+                    content = rows_c if content is None else jnp.where(places[h][c] == j, rows_c, content)
+                cross[j, cut, :] = content
+                cross_send(j, lo, size).start()
+
+        def relay(a, when, i, lo, size):
             zz, s, below, k = arrivals[a]
-            ref = half((zz * across + y) * seqs + s, h)
-            last_s = s == tail[0]
-            i = jnp.where(last_s, 2 * seqs - 1 if h == tail[1] else 2 * seqs - 2, 2 * s + h)
-
-            @pl.when(below)
+            ref = strip((zz * across + y) * seqs + s, lo, size)
+
+            @pl.when(when & below)
             def _():
                 up(ref, k, i, me - across).wait_recv()
 
@@ -356,7 +405,7 @@
                 def _():
                     up(ref, k + 1, i, me + across).start()
 
-            @pl.when(jnp.logical_not(below))
+            @pl.when(when & jnp.logical_not(below))
             def _():
                 down(ref, k, i, me + across).wait_recv()
 
@@ -413,8 +462,10 @@
         for a in range(seqs, total):
             zz, s, _, _ = arrivals[a]
             relay_id(a)
-            order = (1 - tail[1], tail[1]) if a == total - 1 else (0, 1)
-            relay(a, order[0])
+            ending = a == total - 1
+            if not ending:
+                relay(a, s < tail, 2 * s, 0, part)
+                relay(a, s == tail, stride - 2, 0, part)
 
             @pl.when(s == 0)
             def _():
@@ -423,17 +474,22 @@
             queue(y, a, y_peer, last, places)
             if a == total - seqs:
                 id_side(y).start()
+            if not ending:
+                pop(0, a, places)
+                relay(a, s < tail, 2 * s + 1, part, part)
+            for t, (lo, size) in enumerate(pieces):
+                if ending or lo:
+                    relay(a, s == tail, 2 * tail + t, lo, size)
+                if ending:
+                    pop(1 if lo else 0, a, places, [(lo, size)])
+            if not ending:
+                pop(1, a, places)
+            relay_extra(a)
             if a == total - 2:
-                pop(order[0], a, places)
-                relay(a, order[1])
-                pop(order[1], a, places)
-                relay_extra(a)
                 id_side(1 - y).wait_recv()
                 rest = pltpu.make_async_copy(table_all.at[1 - y], table_s.at[1 - y], t_sem.at[2 * depth + 1])
                 rest.start()
                 rest.wait()
-                continue
-            if a == total - 1:
                 found = [[jnp.int32(-1)] * SLOTS for _ in range(2)]
                 peer_last = [jnp.int32(-1), jnp.int32(-1)]
                 peer_places = [[], []]
@@ -446,20 +502,16 @@
                     there = (cz * across + 1 - y) * seqs + cs
                     for h in range(2):
                         place = n * seqs + peer_places[h][c]
-                        if h == tail[1]:
+                        if h == 0:
                             place = jnp.where(is_tail(c), there, place)
                         found[h] = [
                             jnp.where(mine == j, here, jnp.where(theirs == j, place, f))
                             for j, f in enumerate(found[h])
                         ]
                 where_is = found
-            pop(order[0], a, places)
-            relay(a, order[1])
-            pop(order[1], a, places)
-            relay_extra(a)
-        for j in range(slots):
-            for h in range(2):
-                cross_send(j, h).wait_recv()
+                settle(range(depth - 2))
+        for piece_of in all_cross:
+            cross_send(*piece_of).wait_recv()
 
     for h in range(2):
         cut = pl.ds(h * part, part)
@@ -468,21 +520,7 @@
             rows_j = buf[jnp.maximum(index, 0), cut, :]
             out[j, cut, :] = jnp.where(index >= 0, rows_j, jnp.zeros_like(rows_j))
 
-    for s in range(seqs):
-        for c in peer_copies[s]:
-            c.wait_send()
-    for k in range(depth - 1):
-        @pl.when(has_up & (z - k >= 0))
-        def _():
-            id_up(z - k, k, me + across).wait_send()
-            for i in range(len(units)):
-                up(own_unit(me - k * across, i), k, i, me + across).wait_send()
-
-        @pl.when(has_down & (z + k < depth))
-        def _():
-            id_down(z + k, k, me - across).wait_send()
-            for i in range(len(units)):
-                down(own_unit(me + k * across, i), k, i, me - across).wait_send()
+    settle(range(depth - 2, depth - 1) if pair else range(depth - 1))
     if pair:
         @pl.when(has_up)
         def _():
@@ -497,9 +535,8 @@
             tail_side(me).wait_send()
 
         id_side(y).wait_send()
-        for j in range(slots):
-            for h in range(2):
-                cross_send(j, h).wait_send()
+        for piece_of in all_cross:
+            cross_send(*piece_of).wait_send()
 
 
 def solution(mesh):
@@ -517,9 +554,9 @@
         half_dim = HD // 2
         inv_freq = np.power(np.float64(rope_base), -2.0 * np.arange(half_dim) / HD)
         freq = jnp.asarray(np.tile(inv_freq, 2)[None, :].astype(np.float32))
-        stride = (2 * seqs if wide else 1) + 1
+        stride = (2 * seqs + 1 if wide else 1) + 1
         z_sems = pltpu.SemaphoreType.DMA((max(1, (depth - 1) * stride),))
-        y_sems = pltpu.SemaphoreType.DMA((2 * slots + 1,))
+        y_sems = pltpu.SemaphoreType.DMA((3 * slots + 1,))
         vmem = pl.BlockSpec(memory_space=pltpu.VMEM)
         hbm = pl.BlockSpec(memory_space=pltpu.HBM)
         return pl.pallas_call(
@@ -548,6 +585,8 @@
                 pltpu.SemaphoreType.DMA((2 * depth + 1,)),
                 pltpu.SemaphoreType.DMA((2 * depth + 2,)),
                 z_sems, z_sems, z_sems, z_sems, y_sems, y_sems,
+                pltpu.SemaphoreType.REGULAR,
+                pltpu.SemaphoreType.REGULAR,
             ],
             compiler_params=pltpu.CompilerParams(collective_id=0, has_side_effects=True, vmem_limit_bytes=63 * 1000 * 1024),
         )(hidden, norm_gain, w_kv, lengths, page_table.reshape(seqs), freq)

time: 41.1 us -> 40 us (0.973)
  Pallas kernels: 39.9 us -> 38.8 us
    pallas_call x1, Pallas kernels: 39.9 us -> 38.8 us  [per_device(): pl.pallas_call(functools.partial(kernel, depth, across, slots), out_shape...]
where the time goes in v3:
time: 40 us; the launch traced here: 39.8 us
  Pallas kernels  38.8 us (97%)
  local copies, waits for them, and re-layouts  0.97 us (2%)
    pallas_call x1, Pallas kernels, per_device(): pl.pallas_call(functools.partial(kernel, depth, across, slots), out_shape...  38.8 us
    unnamed x1, local copies, waits for them, and re-layouts  0.97 us

profile of v3, /device:TPU:0, one launch (start us, length us, event | category | flops | bytes accessed | tf_op | source)
XLA Modules:
  0.0 39.8 jit_solution(8428148850308233502)
XLA Ops:
  0.0 38.8 %shard_map.64 = bf16[8,128,512]{2,1,0:T(8,128)(2,1)S(1)} custom-call(bf16[3,128,4096]{2,1,0:T(8,128)(2,1)} %hidden.1, bf16[8192]{0:T(1024)(128)(2,1)} %gain_hbm.1, bf16[8192,512]{1,0:T(8,128)(2,1)} %w_kv.1, s32[3]{0:T(128)} %lengths_hbm.1, s32[3]{0:T(128)} %bitcast.1, f32[1,128]{1,0:T(1,128)} %constant.2.clone.freq_hbm), custom_call_target="tpu_custom_call" | custom-call | tf_op jit(solution)/shard_map/pallas_call | solution.py:562
  38.9 1.0 %copy.8 = bf16[8,128,512]{2,1,0:T(8,128)(2,1)} copy(bf16[8,128,512]{2,1,0:T(8,128)(2,1)S(1)} %shard_map.64) | data formatting | bytes 2097152

commit v4 on v3

--- a/solution.py
+++ b/solution.py
@@ -40,6 +40,7 @@
     has_up = z + 1 < depth
     has_down = z >= 1
     pair = across == 2
+    twice = side == 0
 
     own_copies = [pltpu.make_async_copy(hidden.at[s], h_own.at[s], h_sem.at[s]) for s in range(seqs)]
 
@@ -267,7 +268,7 @@
                 def _():
                     pl.semaphore_wait(in_side, 1)
 
-                @pl.when(at_edge)
+                @pl.when(at_edge & twice)
                 def _():
                     tail_side(me).start()
             mine = [i for i, unit in enumerate(units) if unit[0] == s]
@@ -289,15 +290,15 @@
     own_scalar.start()
 
     if pair:
-        @pl.when(at_edge)
+        @pl.when(at_edge & twice)
         def _():
             tail_side(y_peer).wait_recv()
 
-        @pl.when(z == 0)
+        @pl.when((z == 0) & twice)
         def _():
             up(extra_unit(0), 0, stride - 1, me + across).start()
 
-        @pl.when(z == depth - 1)
+        @pl.when((z == depth - 1) & twice)
         def _():
             down(extra_unit(depth - 1), 0, stride - 1, me - across).start()
 
@@ -349,7 +350,7 @@
         total = seqs * depth
         near = jnp.minimum(z, depth - 1 - z)
         below_far = z > depth - 1 - z
-        first_pop = [total - 1 - slots, total - slots]
+        first_pop = [total - slots - twice.astype(jnp.int32), total - slots]
 
         def arrival(a):
             if a < seqs:
@@ -367,7 +368,7 @@
 
         def is_tail(a):
             zz, s, _, _ = arrivals[a]
-            return ((zz == 0) | (zz == depth - 1)) & (s == tail)
+            return ((zz == 0) | (zz == depth - 1)) & (s == tail) & twice
 
         def queue(lane_of, a, target, last, places):
             zz, s, _, _ = arrivals[a]
@@ -375,23 +376,33 @@
             wanted = (page >= target * SLOTS) & (page < target * SLOTS + SLOTS)
             for h in range(2):
                 goes = wanted & jnp.logical_not(is_tail(a)) if h == 0 else wanted
-                place = jnp.maximum(last[h] + 1, max(a - first_pop[h], 0))
+                place = jnp.maximum(last[h] + 1, jnp.maximum(a - first_pop[h], 0))
                 places[h].append(jnp.where(goes, place, -1))
                 last[h] = jnp.where(goes, place, last[h])
 
         def pop(h, a, places, cuts=None):
-            j = a - first_pop[h]
-            if j < 0 or j >= slots:
+            top = a - (total - slots)
+            if top < 0 and (h == 1 or top < -1):
                 return
-            for lo, size in cuts or cross_pieces(h, j):
-                cut = pl.ds(lo, size)
-                content = None
-                for c in range(j, a + 1):
-                    zz, s, _, _ = arrivals[c]
-                    rows_c = buf[(zz * across + y) * seqs + s, cut, :]
-                    content = rows_c if content is None else jnp.where(places[h][c] == j, rows_c, content)
-                cross[j, cut, :] = content
-                cross_send(j, lo, size).start()
+            j = jnp.int32(a) - first_pop[h]
+
+            def fill():
+                for lo, size in cuts or cross_pieces(h, top):
+                    cut = pl.ds(lo, size)
+                    content = None
+                    for c in range(max(top, 0), a + 1):
+                        zz, s, _, _ = arrivals[c]
+                        rows_c = buf[(zz * across + y) * seqs + s, cut, :]
+                        content = rows_c if content is None else jnp.where(places[h][c] == j, rows_c, content)
+                    cross[j, cut, :] = content
+                    cross_send(j, lo, size).start()
+
+            if h == 0 and top < 0:
+                pl.when(twice)(fill)
+            elif h == 0 and a == total - 1:
+                pl.when(jnp.logical_not(twice))(fill)
+            else:
+                fill()
 
         def relay(a, when, i, lo, size):
             zz, s, below, k = arrivals[a]
@@ -522,15 +533,15 @@
 
     settle(range(depth - 2, depth - 1) if pair else range(depth - 1))
     if pair:
-        @pl.when(has_up)
+        @pl.when(has_up & twice)
         def _():
             up(extra_unit(0), z, stride - 1, me + across).wait_send()
 
-        @pl.when(has_down)
+        @pl.when(has_down & twice)
         def _():
             down(extra_unit(depth - 1), depth - 1 - z, stride - 1, me - across).wait_send()
 
-        @pl.when(at_edge)
+        @pl.when(at_edge & twice)
         def _():
             tail_side(me).wait_send()
 

time: 40 us -> 39.8 us (level)
  no operation moved by 1% of the time
where the time goes in v4:
time: 39.8 us; the launch traced here: 39.7 us
  Pallas kernels  38.7 us (97%)
  local copies, waits for them, and re-layouts  0.97 us (2%)
    pallas_call x1, Pallas kernels, per_device(): pl.pallas_call(functools.partial(kernel, depth, across, slots), out_shape...  38.7 us
    unnamed x1, local copies, waits for them, and re-layouts  0.97 us

profile of v4, /device:TPU:0, one launch (start us, length us, event | category | flops | bytes accessed | tf_op | source)
XLA Modules:
  0.0 39.7 jit_solution(6866392850375400611)
XLA Ops:
  0.0 38.7 %shard_map.64 = bf16[8,128,512]{2,1,0:T(8,128)(2,1)S(1)} custom-call(bf16[3,128,4096]{2,1,0:T(8,128)(2,1)} %hidden.1, bf16[8192]{0:T(1024)(128)(2,1)} %gain_hbm.1, bf16[8192,512]{1,0:T(8,128)(2,1)} %w_kv.1, s32[3]{0:T(128)} %lengths_hbm.1, s32[3]{0:T(128)} %bitcast.1, f32[1,128]{1,0:T(1,128)} %constant.2.clone.freq_hbm), custom_call_target="tpu_custom_call" | custom-call | tf_op jit(solution)/shard_map/pallas_call | solution.py:573
  38.7 1.0 %copy.8 = bf16[8,128,512]{2,1,0:T(8,128)(2,1)} copy(bf16[8,128,512]{2,1,0:T(8,128)(2,1)S(1)} %shard_map.64) | data formatting | bytes 2097152
